TPU v7x, 32 devices: a whole 2x2x4 slice. The times are simulated.
32 devices in a mesh: row: 4 (over z), col: 8 (over y, x, core).
Axes of the slice: x: 2, y: 2, z: 4, core: 2. Of those that a mesh axis runs over, the one named last changes fastest.
Arguments:
- tile_data: bfloat16 [8, 4, 8, 2, 128, 128], P(None, 'row', 'col'), may hold values from 0 to 1, as said below
- tile_cols: int32 [8, 4, 8, 2], P(None, 'row', 'col'), may hold values from -1 to 31, as said below
Outputs:
- vertex_triangles: float32 [8, 4, 128], P(None, 'row', 'col')
- triangles: float32 [], replicated
Inputs may be any that keep to these rules, and one draw needn't show every extreme that they name: `tile_cols`: slot (a, r, c, s) holds -1 (empty) or a tile column J with J % 8 == c and J >= a 4 + r; the columns of one tile row are distinct; every slot of tile row 0 is filled; tile row I keeps each slot that has an allowed column with probability (32 - I) / 32, so rows with a lower index hold more tiles on average. `tile_data`: entries are 0 or 1; tiles of empty slots are zero; a tile whose column equals its tile row is strictly upper triangular; about one entry in 8 of a stored tile is 1, with edges clustered among groups of vertices.
All inputs are finite; a program needn't handle non-finite values.
Results may differ from a plain program's by a relative error of at most 0.0003.
Values may be sent and summed in bfloat16 or wider, within the bound.
A program may use at most 128 MiB of HBM per device.

v0:
```python
import jax
import jax.numpy as jnp
from jax import lax
from jax.sharding import PartitionSpec as P

vertex_scale = 2.0 ** (-14)
total_scale = 2.0 ** (-12)


def taken_in(share, axis, dim):

    def gathered(part):
        return lax.all_gather(part, axis, axis=dim, tiled=True)

    return jax.tree.map(gathered, share)


def tile_counts(stored, middle, own_tiles, own_cols, col_tiles, col_index):
    valid = middle >= 0
    clipped = jnp.clip(middle, 0, col_tiles.shape[0] - 1).astype(jnp.int32)
    partner = col_tiles[clipped]
    partner_cols = col_index[clipped]
    matches = partner_cols[:, :, None] == own_cols[None, None, :]
    matches = matches & valid[:, None, None] & (own_cols >= 0)[None, None, :]
    weights = matches.astype(jnp.bfloat16)
    targets = jnp.einsum("pqs,sxz->pqxz", weights, own_tiles, preferred_element_type=jnp.float32)
    paths = jnp.einsum("pxy,pqyz->pqxz", stored, partner, preferred_element_type=jnp.float32)
    return jnp.sum(paths * targets, axis=(0, 1, 3))


def on_device(tile_data, tile_cols):
    rows_here = tile_data.shape[0]
    slots = tile_data.shape[3]
    width = tile_data.shape[4]
    own_tiles = tile_data[:, 0, 0]
    own_cols = tile_cols[:, 0, 0]
    row_index = lax.all_gather(tile_cols, "col", axis=2, tiled=True)
    col_index = lax.all_gather(tile_cols, "row", axis=1, tiled=True)
    col_tiles = lax.all_gather(tile_data, "row", axis=1, tiled=True)
    tile_rows = col_index.shape[0] * col_index.shape[1]
    col_index = col_index.reshape(tile_rows, slots)
    col_tiles = col_tiles.reshape(tile_rows, slots, width, width)

    def add_piece(carry, piece, start):
        devices_here = piece.shape[2]
        middle = lax.dynamic_slice_in_dim(row_index, start.astype(jnp.int32), devices_here, 2)
        middle = middle.reshape(rows_here, devices_here * slots)
        stored = piece.reshape(rows_here, devices_here * slots, width, width)

        def per_row(packed):
            return tile_counts(packed[0], packed[1], packed[2], packed[3], col_tiles, col_index)

        return carry + lax.map(per_row, (stored, middle, own_tiles, own_cols))

    initial = jnp.zeros((rows_here, width), jnp.float32)
    partial_value = add_piece(initial, taken_in(tile_data, "col", 2), jnp.int32(0))
    shares = lax.psum_scatter(
        partial_value.reshape(rows_here, 1, width), "col", scatter_dimension=2, tiled=True
    )
    vertices = tile_rows * width
    overall = lax.psum(jnp.sum(partial_value), ("row", "col"))
    return (shares * vertex_scale, overall * (total_scale / vertices))


def solution(mesh):
    return jax.shard_map(
        on_device,
        mesh=mesh,
        in_specs=(P(None, "row", "col", None, None, None), P(None, "row", "col", None)),
        out_specs=(P(None, "row", "col"), P()),
        check_vma=False,
    )
```

profile of v0, /device:TPU:0, one launch (start us, length us, event | category | flops | bytes accessed | tf_op | source)
XLA Modules:
  0.0 213.6 jit_solution(9713125407251959521)
XLA Ops:
  7.2 0.7 all-gather.3.cloned.1.call-update
  8.0 0.7 all-gather.5.cloned.1.call-update
  8.7 2.4 %copy.37 = bf16[8,1,1,2,128,128]{5,3,4,0,2,1:T(2,128)(2,1)} copy(bf16[8,1,1,2,128,128]{5,4,3,2,1,0:T(8,128)(2,1)} %param.4) | data formatting | bytes 1048576 | tf_op args[0]
  11.1 12.6 %all_gather.15 = s32[8,4,1,2]{0,3,2,1:T(2,128)S(1)} all-gather(s32[8,1,1,2]{0,3,2,1:T(2,128)S(1)} %copy-done.1), channel_id=1, replica_groups=mesh['row'=4,'col'=8] {'row'}, dimensions={1}, use_global_device_ids=true | all-gather | bytes 320 | tf_op jit(solution)/shard_map/all_gather | solution.py:38
  23.9 8.9 %all_gather.12 = s32[8,1,8,2]{0,3,1,2:T(2,128)S(1)} all-gather(s32[8,1,1,2]{0,3,1,2:T(2,128)S(1)} %bitcast.68), channel_id=1, replica_groups=mesh['row'=4,'col'=8] {'col'}, dimensions={2}, use_global_device_ids=true | all-gather | bytes 576 | tf_op jit(solution)/shard_map/all_gather | solution.py:37
  33.0 25.0 %all-gather.3.cloned.1.call-done = bf16[8,4,1,2,128,128]{5,4,3,2,1,0:T(8,128)(2,1)} async-done(((bf16[8,1,1,2,128,128]{5,4,3,2,1,0:T(8,128)(2,1)}), bf16[8,4,1,2,128,128]{5,4,3,2,1,0:T(8,128)(2,1)}) %all-gather.3.cloned.1.call-update) | async-done | bytes 2097168 | tf_op jit(solution)/shard_map/all_gather | solution.py:39
  58.0 37.3 %all-gather.5.cloned.1.call-done = bf16[8,1,8,2,128,128]{5,4,3,2,1,0:T(8,128)(2,1)} async-done(((bf16[8,1,1,2,128,128]{5,4,3,2,1,0:T(8,128)(2,1)}), bf16[8,1,8,2,128,128]{5,4,3,2,1,0:T(8,128)(2,1)}) %all-gather.5.cloned.1.call-update) | async-done | bytes 4194320 | tf_op jit(solution)/shard_map/all_gather | solution.py:13
  95.3 67.3 %while.10 = (s32[]{:T(128)}, f32[8,128]{1,0:T(8,128)S(1)}, s32[8,16]{1,0:T(8,128)S(1)}, bf16[32,2,128,128]{3,2,1,0:T(8,128)(2,1)}, bf16[8,16,128,128]{3,2,1,0:T(...) while((s32[]{:T(128)}, f32[8,128]{1,0:T(8,128)S(1)}, ...), condition=%wide.region_2.3_spmd, body=%wide.region_0.2_spmd.sunk | while | flops 137364624 | bytes 20520652 | solution.py:53
  95.3 0.6 gather_fusion
  96.0 1.4 fusion.32
  97.4 1.8 copy.41
  99.3 2.5 %gather_fusion.1 = bf16[16,2,128,128]{3,2,1,0:T(8,128)(2,1)S(1)} fusion(bf16[32,2,128,128]{3,2,1,0:T(8,128)(2,1)} %get-tuple-element.163, s32[1024]{0:T(1024)S(1)} %pad_clamp_fusion.2), kind=kCustom, calls=%fused_computation.clone.1 | custom fusion | bytes 2097216 | tf_op jit(solution)/shard_map/while/body/eval_jaxpr/gather | solution.py:21
  101.8 1.9 fusion.33
  103.7 0.6 gather_fusion
  104.4 1.4 fusion.32
  105.8 1.8 copy.41
  107.7 2.5 %gather_fusion.1 = bf16[16,2,128,128]{3,2,1,0:T(8,128)(2,1)S(1)} fusion(bf16[32,2,128,128]{3,2,1,0:T(8,128)(2,1)} %get-tuple-element.163, s32[1024]{0:T(1024)S(1)} %pad_clamp_fusion.2), kind=kCustom, calls=%fused_computation.clone.1 | custom fusion | bytes 2097216 | tf_op jit(solution)/shard_map/while/body/eval_jaxpr/gather | solution.py:21
  110.2 1.9 fusion.33
  112.1 0.6 gather_fusion
  112.8 1.4 fusion.32
  114.3 1.8 copy.41
  116.1 2.5 %gather_fusion.1 = bf16[16,2,128,128]{3,2,1,0:T(8,128)(2,1)S(1)} fusion(bf16[32,2,128,128]{3,2,1,0:T(8,128)(2,1)} %get-tuple-element.163, s32[1024]{0:T(1024)S(1)} %pad_clamp_fusion.2), kind=kCustom, calls=%fused_computation.clone.1 | custom fusion | bytes 2097216 | tf_op jit(solution)/shard_map/while/body/eval_jaxpr/gather | solution.py:21
  118.6 1.9 fusion.33
  121.2 1.4 fusion.32
  122.7 1.8 copy.41
  124.5 2.5 %gather_fusion.1 = bf16[16,2,128,128]{3,2,1,0:T(8,128)(2,1)S(1)} fusion(bf16[32,2,128,128]{3,2,1,0:T(8,128)(2,1)} %get-tuple-element.163, s32[1024]{0:T(1024)S(1)} %pad_clamp_fusion.2), kind=kCustom, calls=%fused_computation.clone.1 | custom fusion | bytes 2097216 | tf_op jit(solution)/shard_map/while/body/eval_jaxpr/gather | solution.py:21
  127.0 1.9 fusion.33
  129.6 1.4 fusion.32
  131.1 1.8 copy.41
  132.9 2.5 %gather_fusion.1 = bf16[16,2,128,128]{3,2,1,0:T(8,128)(2,1)S(1)} fusion(bf16[32,2,128,128]{3,2,1,0:T(8,128)(2,1)} %get-tuple-element.163, s32[1024]{0:T(1024)S(1)} %pad_clamp_fusion.2), kind=kCustom, calls=%fused_computation.clone.1 | custom fusion | bytes 2097216 | tf_op jit(solution)/shard_map/while/body/eval_jaxpr/gather | solution.py:21
  135.4 1.9 fusion.33
  138.0 1.4 fusion.32
  139.5 1.8 copy.41
  141.3 2.5 %gather_fusion.1 = bf16[16,2,128,128]{3,2,1,0:T(8,128)(2,1)S(1)} fusion(bf16[32,2,128,128]{3,2,1,0:T(8,128)(2,1)} %get-tuple-element.163, s32[1024]{0:T(1024)S(1)} %pad_clamp_fusion.2), kind=kCustom, calls=%fused_computation.clone.1 | custom fusion | bytes 2097216 | tf_op jit(solution)/shard_map/while/body/eval_jaxpr/gather | solution.py:21
  143.8 1.9 fusion.33
  146.4 1.4 fusion.32
  147.9 1.8 copy.41
  149.7 2.5 %gather_fusion.1 = bf16[16,2,128,128]{3,2,1,0:T(8,128)(2,1)S(1)} fusion(bf16[32,2,128,128]{3,2,1,0:T(8,128)(2,1)} %get-tuple-element.163, s32[1024]{0:T(1024)S(1)} %pad_clamp_fusion.2), kind=kCustom, calls=%fused_computation.clone.1 | custom fusion | bytes 2097216 | tf_op jit(solution)/shard_map/while/body/eval_jaxpr/gather | solution.py:21
  152.2 1.9 fusion.33
  154.9 1.4 fusion.32
  156.3 1.8 copy.41
  158.2 2.5 %gather_fusion.1 = bf16[16,2,128,128]{3,2,1,0:T(8,128)(2,1)S(1)} fusion(bf16[32,2,128,128]{3,2,1,0:T(8,128)(2,1)} %get-tuple-element.163, s32[1024]{0:T(1024)S(1)} %pad_clamp_fusion.2), kind=kCustom, calls=%fused_computation.clone.1 | custom fusion | bytes 2097216 | tf_op jit(solution)/shard_map/while/body/eval_jaxpr/gather | solution.py:21
  160.7 1.9 fusion.33
  162.8 0.8 bitcast_reduce_fusion
  163.7 0.6 reduce_sum.18
  164.3 39.5 %psum.7 = f32[]{:T(128)} all-reduce(f32[]{:T(128)} %reduce_sum.18), channel_id=1, replica_groups=mesh['row'=4,'col'=8] {'row','col'}, use_global_device_ids=true, to_apply=%region_5.6 | all-reduce | flops 1 | bytes 8 | tf_op jit(solution)/shard_map/psum | solution.py:61
  204.4 0.8 reshape_bitcast_fusion
  205.3 0.6 broadcast_multiply_fusion
  (82 shorter events, 4.9 us)
Async XLA Ops:
  7.2 4.0 %copy-start.1 = (s32[8,1,1,2]{0,3,2,1:T(2,128)S(1)}, s32[8,1,1,2]{0,3,2,1:T(2,128)}, u32[]{:S(2)}) copy-start(s32[8,1,1,2]{0,3,2,1:T(2,128)} %param.5) | copy-start | bytes 196
  7.2 50.8 %all-gather.3.cloned.1.call-start = ((), (), s32[]{:S(2)}) async-start(), calls=%async_computation.1 | async-start | bytes 2621440 | tf_op jit(solution)/shard_map/all_gather | solution.py:39
  7.9 87.4 %all-gather.5.cloned.1.call-start = ((), (), s32[]{:S(2)}) async-start(), calls=%async_computation.2 | async-start | bytes 4718592 | tf_op jit(solution)/shard_map/all_gather | solution.py:13
  8.7 195.8 %reduce-scatter.4.cloned.1.call-start = ((), (), s32[]{:S(2)}) async-start(), calls=%async_computation.3 | async-start | bytes 73728
  99.3 2.5 %copy-start = (f32[16,2,128,128]{2,3,1,0:T(8,128)S(1)}, f32[16,2,128,128]{2,3,1,0:T(8,128)}, u32[]{:S(2)}) copy-start(f32[16,2,128,128]{2,3,1,0:T(8,128)} %copy.41) | copy-start | bytes 6291460 | tf_op jit(solution)/shard_map/while
  107.7 2.5 %copy-start = (f32[16,2,128,128]{2,3,1,0:T(8,128)S(1)}, f32[16,2,128,128]{2,3,1,0:T(8,128)}, u32[]{:S(2)}) copy-start(f32[16,2,128,128]{2,3,1,0:T(8,128)} %copy.41) | copy-start | bytes 6291460 | tf_op jit(solution)/shard_map/while
  116.1 2.5 %copy-start = (f32[16,2,128,128]{2,3,1,0:T(8,128)S(1)}, f32[16,2,128,128]{2,3,1,0:T(8,128)}, u32[]{:S(2)}) copy-start(f32[16,2,128,128]{2,3,1,0:T(8,128)} %copy.41) | copy-start | bytes 6291460 | tf_op jit(solution)/shard_map/while
  124.5 2.5 %copy-start = (f32[16,2,128,128]{2,3,1,0:T(8,128)S(1)}, f32[16,2,128,128]{2,3,1,0:T(8,128)}, u32[]{:S(2)}) copy-start(f32[16,2,128,128]{2,3,1,0:T(8,128)} %copy.41) | copy-start | bytes 6291460 | tf_op jit(solution)/shard_map/while
  132.9 2.5 %copy-start = (f32[16,2,128,128]{2,3,1,0:T(8,128)S(1)}, f32[16,2,128,128]{2,3,1,0:T(8,128)}, u32[]{:S(2)}) copy-start(f32[16,2,128,128]{2,3,1,0:T(8,128)} %copy.41) | copy-start | bytes 6291460 | tf_op jit(solution)/shard_map/while
  141.3 2.5 %copy-start = (f32[16,2,128,128]{2,3,1,0:T(8,128)S(1)}, f32[16,2,128,128]{2,3,1,0:T(8,128)}, u32[]{:S(2)}) copy-start(f32[16,2,128,128]{2,3,1,0:T(8,128)} %copy.41) | copy-start | bytes 6291460 | tf_op jit(solution)/shard_map/while
  149.7 2.5 %copy-start = (f32[16,2,128,128]{2,3,1,0:T(8,128)S(1)}, f32[16,2,128,128]{2,3,1,0:T(8,128)}, u32[]{:S(2)}) copy-start(f32[16,2,128,128]{2,3,1,0:T(8,128)} %copy.41) | copy-start | bytes 6291460 | tf_op jit(solution)/shard_map/while
  158.2 2.5 %copy-start = (f32[16,2,128,128]{2,3,1,0:T(8,128)S(1)}, f32[16,2,128,128]{2,3,1,0:T(8,128)}, u32[]{:S(2)}) copy-start(f32[16,2,128,128]{2,3,1,0:T(8,128)} %copy.41) | copy-start | bytes 6291460 | tf_op jit(solution)/shard_map/while
Sparse Core Ops, SparseCore 0:
  9.6 48.3 all-gather.2
  59.9 35.3 all-gather.4
  163.8 33.5 reduce-scatter.3
where the time goes:
time: 215 us; the launch traced here: 214 us
  waiting for transfers between devices  63.7 us (30%)
  blocking collectives  61 us (28%)
  local copies, waits for them, and re-layouts  44.8 us (21%)
  matrix products  26.4 us (12%)
  between operations  15.6 us (7%)
    psum x1, blocking collectives, on_device(): overall = lax.psum(jnp.sum(partial_value), ('row', 'col'))  39.5 us
    all_gather x1, waiting for transfers between devices, gathered(): return lax.all_gather(part, axis, axis=dim, tiled=True)  37.3 us
    all_gather x1, waiting for transfers between devices, on_device(): col_tiles = lax.all_gather(tile_data, 'row', axis=1, tiled=True)  25 us
    gather x8, local copies, waits for them, and re-layouts, tile_counts(): partner = col_tiles[clipped]  19.9 us
    dot_general x8, matrix products, tile_counts(): jnp.einsum('pxy,pqyz->pqxz', stored, partner, preferred_element_type=jnp....  14.9 us
    dot_general x8, local copies, waits for them, and re-layouts, tile_counts(): jnp.einsum('pqs,sxz->pqxz', weights, own_tiles, preferred_element_type=jn...  14.7 us
    all_gather x1, blocking collectives, on_device(): col_index = lax.all_gather(tile_cols, 'row', axis=1, tiled=True)  12.6 us
    dot_general x8, matrix products, tile_counts(): jnp.einsum('pqs,sxz->pqxz', weights, own_tiles, preferred_element_type=jn...  11.5 us
  transfers between devices with their start and end apart: 3, of which 2 were waited for; matrix products, arithmetic and copies ran while one was open for 2% of the time, Pallas kernels for 0%

commit v1 on v0

--- a/solution.py
+++ b/solution.py
@@ -36,7 +36,12 @@
     own_cols = tile_cols[:, 0, 0]
     row_index = lax.all_gather(tile_cols, "col", axis=2, tiled=True)
     col_index = lax.all_gather(tile_cols, "row", axis=1, tiled=True)
-    col_tiles = lax.all_gather(tile_data, "row", axis=1, tiled=True)
+    ring = [tile_data]
+    for hop in range(3):
+        ring.append(lax.ppermute(ring[-1], "row", [(dev, (dev + 1) % 4) for dev in range(4)]))
+    col_tiles = jnp.roll(
+        jnp.concatenate(ring[::-1], axis=1), (lax.axis_index("row") + 1) * ring[0].shape[1], axis=1
+    )
     tile_rows = col_index.shape[0] * col_index.shape[1]
     col_index = col_index.reshape(tile_rows, slots)
     col_tiles = col_tiles.reshape(tile_rows, slots, width, width)

time: 215 us -> 185 us (0.86)
  waiting for transfers between devices: 63.7 us -> 29.8 us
  starting transfers between devices: 0.11 us -> 3.19 us
    all_gather x1, waiting for transfers between devices: 37.3 us -> 0.01 us  [gathered(): return lax.all_gather(part, axis, axis=dim, tiled=True)]
    ppermute x0 -> x3, waiting for transfers between devices: none -> 29 us  [on_device(): lax.ppermute(ring[-1], 'row', [(dev, (dev + 1) % 4) for dev in range(4)])]
    all_gather x1 -> x0, waiting for transfers between devices: 25 us -> none  [on_device(): col_tiles = lax.all_gather(tile_data, 'row', axis=1, tiled=True)]
    dot_general x8, matrix products: 11.5 us -> 4.81 us  [tile_counts(): jnp.einsum('pqs,sxz->pqxz', weights, own_tiles, preferred_element_type=jn...]
    dot_general x8, matrix products: 14.9 us -> 20.7 us  [tile_counts(): jnp.einsum('pxy,pqyz->pqxz', stored, partner, preferred_element_type=jnp....]
    ppermute x0 -> x3, starting transfers between devices: none -> 3.11 us  [on_device(): lax.ppermute(ring[-1], 'row', [(dev, (dev + 1) % 4) for dev in range(4)])]
    unnamed x7 -> x14, local copies, waits for them, and re-layouts: 4.42 us -> 4.06 us
  transfers between devices with their start and end apart: 3 -> 5, of which waited for: 2 -> 2; matrix products, arithmetic and copies ran while one was open for 2% -> 3% of each run, Pallas kernels for 0% -> 0%
where the time goes in v1:
time: 185 us; the launch traced here: 184 us
  blocking collectives  62.6 us (34%)
  local copies, waits for them, and re-layouts  45.4 us (25%)
  waiting for transfers between devices  29.8 us (16%)
  matrix products  25.5 us (14%)
  between operations  16 us (9%)
  starting transfers between devices  3.19 us (2%)
    psum x1, blocking collectives, on_device(): overall = lax.psum(jnp.sum(partial_value), ('row', 'col'))  39.6 us
    ppermute x3, waiting for transfers between devices, on_device(): lax.ppermute(ring[-1], 'row', [(dev, (dev + 1) % 4) for dev in range(4)])  29 us
    dot_general x8, matrix products, tile_counts(): jnp.einsum('pxy,pqyz->pqxz', stored, partner, preferred_element_type=jnp....  20.7 us
    gather x8, local copies, waits for them, and re-layouts, tile_counts(): partner = col_tiles[clipped]  18.7 us
    dot_general x8, local copies, waits for them, and re-layouts, tile_counts(): jnp.einsum('pqs,sxz->pqxz', weights, own_tiles, preferred_element_type=jn...  14.7 us
    all_gather x1, blocking collectives, on_device(): col_index = lax.all_gather(tile_cols, 'row', axis=1, tiled=True)  14.3 us
    all_gather x1, blocking collectives, on_device(): row_index = lax.all_gather(tile_cols, 'col', axis=2, tiled=True)  8.63 us
    gather x16, local copies, waits for them, and re-layouts, tile_counts(): partner_cols = col_index[clipped]  5.15 us
  transfers between devices with their start and end apart: 5, of which 2 were waited for; matrix products, arithmetic and copies ran while one was open for 3% of the time, Pallas kernels for 0%

profile of v1, /device:TPU:0, one launch (start us, length us, event | category | flops | bytes accessed | tf_op | source)
XLA Modules:
  0.0 184.3 jit_solution(2837086428151928363)
XLA Ops:
  7.2 0.7 all-gather.2.cloned.1.call-update
  8.0 3.1 %collective-permute-start = (bf16[8,1,1,2,128,128]{5,4,3,2,1,0:T(8,128)(2,1)}, bf16[8,1,1,2,128,128]{5,4,3,2,1,0:T(8,128)(2,1)S(1)}, u32[]{:S(2)}, u32[]{:S(2)}) collective-permute-start(bf16[8,1,1,2,128,128]{5,4,3,2,1,0:T(8,128)(2,1)} %param.4), channel_id=1, source_target_pairs={{0,8},{8,16},{16,24},{24,0},{1,9},{9,17},{17,25},{25,1},{2,10},{10... | collective-permute-start | bytes 1572872 | tf_op jit(solution)/shard_map/ppermute | solution.py:41
  11.1 14.2 %collective-permute-done = bf16[8,1,1,2,128,128]{5,4,3,2,1,0:T(8,128)(2,1)S(1)} collective-permute-done((bf16[8,1,1,2,128,128]{5,4,3,2,1,0:T(8,128)(2,1)}, bf16[8,1,1,2,128,128]{5,4,3,2,1,0:T(8,128)(2,1)S(1)}, u32[]{:S(2)}, u32[]{:S(2)}) %collective-permute-start) | collective-permute-done | bytes 524320 | tf_op jit(solution)/shard_map/ppermute | solution.py:41
  25.2 14.9 %collective-permute-done.1 = bf16[8,1,1,2,128,128]{5,4,3,2,1,0:T(8,128)(2,1)S(1)} collective-permute-done((bf16[8,1,1,2,128,128]{5,4,3,2,1,0:T(8,128)(2,1)S(1)}, bf16[8,1,1,2,128,128]{5,4,3,2,1,0:T(8,128)(2,1)S(1)}, u32[]{:S(2)}, u32[]{:S(2)}) %collective-permute-start.1) | collective-permute-done | bytes 524320 | tf_op jit(solution)/shard_map/ppermute | solution.py:41
  40.1 1.6 copy.37
  41.7 14.3 %all_gather.11 = s32[8,4,1,2]{0,3,2,1:T(2,128)S(1)} all-gather(s32[8,1,1,2]{0,3,2,1:T(2,128)} %param.5), channel_id=1, replica_groups=mesh['row'=4,'col'=8] {'row'}, dimensions={1}, use_global_device_ids=true | all-gather | bytes 320 | tf_op jit(solution)/shard_map/all_gather | solution.py:38
  56.1 8.6 %all_gather.9 = s32[8,1,8,2]{0,3,1,2:T(2,128)S(1)} all-gather(s32[8,1,1,2]{0,3,1,2:T(2,128)} %bitcast.69), channel_id=1, replica_groups=mesh['row'=4,'col'=8] {'col'}, dimensions={2}, use_global_device_ids=true | all-gather | bytes 576 | tf_op jit(solution)/shard_map/all_gather | solution.py:37
  64.8 0.8 copy.28
  66.2 1.5 constant_dynamic-slice_fusion.2
  67.7 65.1 %while.10 = (s32[]{:T(128)}, f32[8,128]{1,0:T(8,128)S(1)}, s32[8,16]{1,0:T(8,128)S(1)}, bf16[32,2,128,128]{3,2,1,0:T(8,128)(2,1)}, bf16[8,16,128,128]{3,2,1,0:T(...) while((s32[]{:T(128)}, f32[8,128]{1,0:T(8,128)S(1)}, ...), condition=%wide.region_2.3_spmd, body=%wide.region_0.2_spmd.sunk | while | flops 137364624 | bytes 12133915 | solution.py:58
  68.4 0.6 fusion.32
  69.0 1.8 %copy.41 = f32[16,2,128,128]{2,3,1,0:T(8,128)} copy(f32[16,2,128,128]{3,0,2,1:T(8,128)S(1)} %fusion.32) | data formatting | bytes 4194304 | tf_op jit(solution)/shard_map/while/body/eval_jaxpr/pqs,sxz->pqxz/dot_general | solution.py:26
  70.8 2.3 %gather_fusion.1 = bf16[16,2,128,128]{3,2,1,0:T(8,128)(2,1)S(1)} fusion(bf16[32,2,128,128]{3,2,1,0:T(8,128)(2,1)} %get-tuple-element.163, s32[1024]{0:T(1024)S(1)} %pad_clamp_fusion.2), kind=kCustom, calls=%fused_computation.clone.1 | custom fusion | bytes 2097216 | tf_op jit(solution)/shard_map/while/body/eval_jaxpr/gather | solution.py:21
  73.2 2.6 %fusion.33 = f32[128]{0:T(128)S(1)} fusion(f32[16,2,128,128]{2,3,1,0:T(8,128)} %copy.41, bf16[16,2,128,128]{3,2,1,0:T(8,128)(2,1)S(1)} %gather_fusion.1, bf16[8,16,128,128]{3,2,1,0:T(8,128)(2,1)} %get-tuple-element.164, s32[]{:T(128)} %get-tuple-element.150), kind=kOutput, calls=%fused_computation.3.clone.1 | convolution fusion | flops 135266176 | bytes 3671040 | tf_op jit(solution)/shard_map/while/body/eval_jaxpr/pxy,pqyz->pqxz/dot_general | solution.py:27
  76.5 0.6 fusion.32
  77.1 1.8 %copy.41 = f32[16,2,128,128]{2,3,1,0:T(8,128)} copy(f32[16,2,128,128]{3,0,2,1:T(8,128)S(1)} %fusion.32) | data formatting | bytes 4194304 | tf_op jit(solution)/shard_map/while/body/eval_jaxpr/pqs,sxz->pqxz/dot_general | solution.py:26
  79.0 2.3 %gather_fusion.1 = bf16[16,2,128,128]{3,2,1,0:T(8,128)(2,1)S(1)} fusion(bf16[32,2,128,128]{3,2,1,0:T(8,128)(2,1)} %get-tuple-element.163, s32[1024]{0:T(1024)S(1)} %pad_clamp_fusion.2), kind=kCustom, calls=%fused_computation.clone.1 | custom fusion | bytes 2097216 | tf_op jit(solution)/shard_map/while/body/eval_jaxpr/gather | solution.py:21
  81.3 2.6 %fusion.33 = f32[128]{0:T(128)S(1)} fusion(f32[16,2,128,128]{2,3,1,0:T(8,128)} %copy.41, bf16[16,2,128,128]{3,2,1,0:T(8,128)(2,1)S(1)} %gather_fusion.1, bf16[8,16,128,128]{3,2,1,0:T(8,128)(2,1)} %get-tuple-element.164, s32[]{:T(128)} %get-tuple-element.150), kind=kOutput, calls=%fused_computation.3.clone.1 | convolution fusion | flops 135266176 | bytes 3671040 | tf_op jit(solution)/shard_map/while/body/eval_jaxpr/pxy,pqyz->pqxz/dot_general | solution.py:27
  84.6 0.6 fusion.32
  85.2 1.8 %copy.41 = f32[16,2,128,128]{2,3,1,0:T(8,128)} copy(f32[16,2,128,128]{3,0,2,1:T(8,128)S(1)} %fusion.32) | data formatting | bytes 4194304 | tf_op jit(solution)/shard_map/while/body/eval_jaxpr/pqs,sxz->pqxz/dot_general | solution.py:26
  87.1 2.3 %gather_fusion.1 = bf16[16,2,128,128]{3,2,1,0:T(8,128)(2,1)S(1)} fusion(bf16[32,2,128,128]{3,2,1,0:T(8,128)(2,1)} %get-tuple-element.163, s32[1024]{0:T(1024)S(1)} %pad_clamp_fusion.2), kind=kCustom, calls=%fused_computation.clone.1 | custom fusion | bytes 2097216 | tf_op jit(solution)/shard_map/while/body/eval_jaxpr/gather | solution.py:21
  89.4 2.6 %fusion.33 = f32[128]{0:T(128)S(1)} fusion(f32[16,2,128,128]{2,3,1,0:T(8,128)} %copy.41, bf16[16,2,128,128]{3,2,1,0:T(8,128)(2,1)S(1)} %gather_fusion.1, bf16[8,16,128,128]{3,2,1,0:T(8,128)(2,1)} %get-tuple-element.164, s32[]{:T(128)} %get-tuple-element.150), kind=kOutput, calls=%fused_computation.3.clone.1 | convolution fusion | flops 135266176 | bytes 3671040 | tf_op jit(solution)/shard_map/while/body/eval_jaxpr/pxy,pqyz->pqxz/dot_general | solution.py:27
  92.1 0.6 gather_fusion
  92.8 0.6 fusion.32
  93.4 1.8 %copy.41 = f32[16,2,128,128]{2,3,1,0:T(8,128)} copy(f32[16,2,128,128]{3,0,2,1:T(8,128)S(1)} %fusion.32) | data formatting | bytes 4194304 | tf_op jit(solution)/shard_map/while/body/eval_jaxpr/pqs,sxz->pqxz/dot_general | solution.py:26
  95.2 2.3 %gather_fusion.1 = bf16[16,2,128,128]{3,2,1,0:T(8,128)(2,1)S(1)} fusion(bf16[32,2,128,128]{3,2,1,0:T(8,128)(2,1)} %get-tuple-element.163, s32[1024]{0:T(1024)S(1)} %pad_clamp_fusion.2), kind=kCustom, calls=%fused_computation.clone.1 | custom fusion | bytes 2097216 | tf_op jit(solution)/shard_map/while/body/eval_jaxpr/gather | solution.py:21
  97.6 2.6 %fusion.33 = f32[128]{0:T(128)S(1)} fusion(f32[16,2,128,128]{2,3,1,0:T(8,128)} %copy.41, bf16[16,2,128,128]{3,2,1,0:T(8,128)(2,1)S(1)} %gather_fusion.1, bf16[8,16,128,128]{3,2,1,0:T(8,128)(2,1)} %get-tuple-element.164, s32[]{:T(128)} %get-tuple-element.150), kind=kOutput, calls=%fused_computation.3.clone.1 | convolution fusion | flops 135266176 | bytes 3671040 | tf_op jit(solution)/shard_map/while/body/eval_jaxpr/pxy,pqyz->pqxz/dot_general | solution.py:27
  100.9 0.6 fusion.32
  101.5 1.8 %copy.41 = f32[16,2,128,128]{2,3,1,0:T(8,128)} copy(f32[16,2,128,128]{3,0,2,1:T(8,128)S(1)} %fusion.32) | data formatting | bytes 4194304 | tf_op jit(solution)/shard_map/while/body/eval_jaxpr/pqs,sxz->pqxz/dot_general | solution.py:26
  103.4 2.3 %gather_fusion.1 = bf16[16,2,128,128]{3,2,1,0:T(8,128)(2,1)S(1)} fusion(bf16[32,2,128,128]{3,2,1,0:T(8,128)(2,1)} %get-tuple-element.163, s32[1024]{0:T(1024)S(1)} %pad_clamp_fusion.2), kind=kCustom, calls=%fused_computation.clone.1 | custom fusion | bytes 2097216 | tf_op jit(solution)/shard_map/while/body/eval_jaxpr/gather | solution.py:21
  105.7 2.6 %fusion.33 = f32[128]{0:T(128)S(1)} fusion(f32[16,2,128,128]{2,3,1,0:T(8,128)} %copy.41, bf16[16,2,128,128]{3,2,1,0:T(8,128)(2,1)S(1)} %gather_fusion.1, bf16[8,16,128,128]{3,2,1,0:T(8,128)(2,1)} %get-tuple-element.164, s32[]{:T(128)} %get-tuple-element.150), kind=kOutput, calls=%fused_computation.3.clone.1 | convolution fusion | flops 135266176 | bytes 3671040 | tf_op jit(solution)/shard_map/while/body/eval_jaxpr/pxy,pqyz->pqxz/dot_general | solution.py:27
  109.0 0.6 fusion.32
  109.7 1.8 %copy.41 = f32[16,2,128,128]{2,3,1,0:T(8,128)} copy(f32[16,2,128,128]{3,0,2,1:T(8,128)S(1)} %fusion.32) | data formatting | bytes 4194304 | tf_op jit(solution)/shard_map/while/body/eval_jaxpr/pqs,sxz->pqxz/dot_general | solution.py:26
  111.5 2.3 %gather_fusion.1 = bf16[16,2,128,128]{3,2,1,0:T(8,128)(2,1)S(1)} fusion(bf16[32,2,128,128]{3,2,1,0:T(8,128)(2,1)} %get-tuple-element.163, s32[1024]{0:T(1024)S(1)} %pad_clamp_fusion.2), kind=kCustom, calls=%fused_computation.clone.1 | custom fusion | bytes 2097216 | tf_op jit(solution)/shard_map/while/body/eval_jaxpr/gather | solution.py:21
  113.8 2.6 %fusion.33 = f32[128]{0:T(128)S(1)} fusion(f32[16,2,128,128]{2,3,1,0:T(8,128)} %copy.41, bf16[16,2,128,128]{3,2,1,0:T(8,128)(2,1)S(1)} %gather_fusion.1, bf16[8,16,128,128]{3,2,1,0:T(8,128)(2,1)} %get-tuple-element.164, s32[]{:T(128)} %get-tuple-element.150), kind=kOutput, calls=%fused_computation.3.clone.1 | convolution fusion | flops 135266176 | bytes 3671040 | tf_op jit(solution)/shard_map/while/body/eval_jaxpr/pxy,pqyz->pqxz/dot_general | solution.py:27
  117.2 0.6 fusion.32
  117.8 1.8 %copy.41 = f32[16,2,128,128]{2,3,1,0:T(8,128)} copy(f32[16,2,128,128]{3,0,2,1:T(8,128)S(1)} %fusion.32) | data formatting | bytes 4194304 | tf_op jit(solution)/shard_map/while/body/eval_jaxpr/pqs,sxz->pqxz/dot_general | solution.py:26
  119.6 2.3 %gather_fusion.1 = bf16[16,2,128,128]{3,2,1,0:T(8,128)(2,1)S(1)} fusion(bf16[32,2,128,128]{3,2,1,0:T(8,128)(2,1)} %get-tuple-element.163, s32[1024]{0:T(1024)S(1)} %pad_clamp_fusion.2), kind=kCustom, calls=%fused_computation.clone.1 | custom fusion | bytes 2097216 | tf_op jit(solution)/shard_map/while/body/eval_jaxpr/gather | solution.py:21
  122.0 2.6 %fusion.33 = f32[128]{0:T(128)S(1)} fusion(f32[16,2,128,128]{2,3,1,0:T(8,128)} %copy.41, bf16[16,2,128,128]{3,2,1,0:T(8,128)(2,1)S(1)} %gather_fusion.1, bf16[8,16,128,128]{3,2,1,0:T(8,128)(2,1)} %get-tuple-element.164, s32[]{:T(128)} %get-tuple-element.150), kind=kOutput, calls=%fused_computation.3.clone.1 | convolution fusion | flops 135266176 | bytes 3671040 | tf_op jit(solution)/shard_map/while/body/eval_jaxpr/pxy,pqyz->pqxz/dot_general | solution.py:27
  125.3 0.6 fusion.32
  125.9 1.8 %copy.41 = f32[16,2,128,128]{2,3,1,0:T(8,128)} copy(f32[16,2,128,128]{3,0,2,1:T(8,128)S(1)} %fusion.32) | data formatting | bytes 4194304 | tf_op jit(solution)/shard_map/while/body/eval_jaxpr/pqs,sxz->pqxz/dot_general | solution.py:26
  127.8 2.3 %gather_fusion.1 = bf16[16,2,128,128]{3,2,1,0:T(8,128)(2,1)S(1)} fusion(bf16[32,2,128,128]{3,2,1,0:T(8,128)(2,1)} %get-tuple-element.163, s32[1024]{0:T(1024)S(1)} %pad_clamp_fusion.2), kind=kCustom, calls=%fused_computation.clone.1 | custom fusion | bytes 2097216 | tf_op jit(solution)/shard_map/while/body/eval_jaxpr/gather | solution.py:21
  130.1 2.6 %fusion.33 = f32[128]{0:T(128)S(1)} fusion(f32[16,2,128,128]{2,3,1,0:T(8,128)} %copy.41, bf16[16,2,128,128]{3,2,1,0:T(8,128)(2,1)S(1)} %gather_fusion.1, bf16[8,16,128,128]{3,2,1,0:T(8,128)(2,1)} %get-tuple-element.164, s32[]{:T(128)} %get-tuple-element.150), kind=kOutput, calls=%fused_computation.3.clone.1 | convolution fusion | flops 135266176 | bytes 3671040 | tf_op jit(solution)/shard_map/while/body/eval_jaxpr/pxy,pqyz->pqxz/dot_general | solution.py:27
  133.0 0.8 bitcast_reduce_fusion
  133.9 0.6 reduce_sum.18
  134.5 39.6 %psum.7 = f32[]{:T(128)} all-reduce(f32[]{:T(128)} %reduce_sum.18), channel_id=1, replica_groups=mesh['row'=4,'col'=8] {'row','col'}, use_global_device_ids=true, to_apply=%region_5.6 | all-reduce | flops 1 | bytes 8 | tf_op jit(solution)/shard_map/psum | solution.py:66
  174.8 0.8 reshape_bitcast_fusion
  175.7 0.6 broadcast_multiply_fusion
  (78 shorter events, 6.4 us)
Async XLA Ops:
  7.2 58.6 %copy-start = (bf16[8,1,1,2,128,128]{5,4,3,2,1,0:T(8,128)(2,1)S(1)}, bf16[8,1,1,2,128,128]{5,4,3,2,1,0:T(8,128)(2,1)}, u32[]{:S(2)}) copy-start(bf16[8,1,1,2,128,128]{5,4,3,2,1,0:T(8,128)(2,1)} %param.4) | copy-start | bytes 1572868
  7.2 60.5 %all-gather.2.cloned.1.call-start = ((), (), s32[]{:S(2)}) async-start(), calls=%async_computation.1 | async-start | bytes 4718592 | tf_op jit(solution)/shard_map/all_gather | solution.py:13
  7.9 166.9 %reduce-scatter.4.cloned.1.call-start = ((), (), s32[]{:S(2)}) async-start(), calls=%async_computation.2 | async-start | bytes 73728
  8.0 17.3 %collective-permute-start = (bf16[8,1,1,2,128,128]{5,4,3,2,1,0:T(8,128)(2,1)}, bf16[8,1,1,2,128,128]{5,4,3,2,1,0:T(8,128)(2,1)S(1)}, u32[]{:S(2)}, u32[]{:S(2)}) collective-permute-start(bf16[8,1,1,2,128,128]{5,4,3,2,1,0:T(8,128)(2,1)} %param.4), channel_id=1, source_target_pairs={{0,8},{8,16},{16,24},{24,0},{1,9},{9,17},{17,25},{25,1},{2,10},{10... | collective-permute-start | bytes 1572872 | tf_op jit(solution)/shard_map/ppermute | solution.py:41
  25.2 14.9 %collective-permute-start.1 = (bf16[8,1,1,2,128,128]{5,4,3,2,1,0:T(8,128)(2,1)S(1)}, bf16[8,1,1,2,128,128]{5,4,3,2,1,0:T(8,128)(2,1)S(1)}, u32[]{:S(2)}, u32[]{:S(2)}) collective-permute-start(bf16[8,1,1,2,128,128]{5,4,3,2,1,0:T(8,128)(2,1)S(1)} %collective-permute-done), channel_id=1, source_target_pairs={{0,8},{8,16},{16,24},{24,0},{1,9},{9,17},{17,25},{25,1},{2,10},{10... | collective-permute-start | bytes 1572872 | tf_op jit(solution)/shard_map/ppermute | solution.py:41
  40.1 25.5 %collective-permute-start.2 = (bf16[8,1,1,2,128,128]{5,4,3,2,1,0:T(8,128)(2,1)S(1)}, bf16[8,1,1,2,128,128]{5,4,3,2,1,0:T(8,128)(2,1)S(1)}, u32[]{:S(2)}, u32[]{:S(2)}) collective-permute-start(bf16[8,1,1,2,128,128]{5,4,3,2,1,0:T(8,128)(2,1)S(1)} %collective-permute-done.1), channel_id=1, source_target_pairs={{0,8},{8,16},{16,24},{24,0},{1,9},{9,17},{17,25},{25,1},{2,10},{10... | collective-permute-start | bytes 1572872 | tf_op jit(solution)/shard_map/ppermute | solution.py:41
Sparse Core Ops, SparseCore 0:
  9.9 39.2 all-gather.1
  134.0 31.8 reduce-scatter.3
